TPU v7x, 32 devices: a whole 2x2x4 slice. The times are simulated.
32 devices in a mesh: grp: 4 (over z), pair: 8 (over y, x, core).
Axes of the slice: x: 2, y: 2, z: 4, core: 2. Of those that a mesh axis runs over, the one named last changes fastest.
Arguments:
- amplitudes: bfloat16 [64, 512, 512], P('pair', 'grp'), may hold values from -6 to 6
- cholesky: bfloat16 [512, 512, 2048], P('pair', 'grp'), may hold values from -0.09375 to 0.09375
Outputs:
- ladder_term: float32 [512, 4, 64], P('pair', None, 'grp')
All inputs are finite; a program needn't handle non-finite values.
Results may differ from a plain program's by a relative error of at most 0.003.
Values may be sent and summed in bfloat16 or wider, within the bound.
A program may use at most 128 MiB of HBM per device.

v0:
```python
import jax
import jax.numpy as jnp
from jax import lax
from jax.sharding import PartitionSpec as P

A_WIN = 4


def spread(value, axis, source):
    kept = jnp.where(lax.axis_index(axis) == source, value, 0).astype(value.dtype)
    return lax.psum(kept, axis)


def build_tile(chol_local, portion):
    return lax.dot_general(
        chol_local, portion, (((2,), (2,)), ((), ())), preferred_element_type=jnp.float32
    ).astype(jnp.bfloat16)


def ladder(integrals, amp_part):
    return lax.dot_general(
        integrals, amp_part, (((1, 3), (1, 2)), ((), ())), preferred_element_type=jnp.float32
    )


def per_device(amplitudes, cholesky):
    own_window = cholesky[:A_WIN]
    everyone = lax.all_gather(amplitudes, "pair", axis=0, tiled=True)
    shared = spread(own_window, "pair", 0)
    summed = ladder(
        build_tile(cholesky, lax.all_gather(shared, "grp", axis=1, tiled=True)), everyone
    )
    return lax.psum_scatter(summed, "grp", scatter_dimension=2, tiled=True)


def solution(mesh):
    in_specs = (P("pair", "grp", None), P("pair", "grp", None))
    out_specs = P("pair", None, "grp")
    return jax.shard_map(
        per_device, mesh=mesh, in_specs=in_specs, out_specs=out_specs, check_vma=False
    )
```

profile of v0, /device:TPU:0, one launch (start us, length us, event | category | flops | bytes accessed | tf_op | source)
XLA Modules:
  0.0 360.8 jit_solution(16896979740591227450)
XLA Ops:
  6.5 0.0 copy-start
  6.5 0.0 all-reduce.2.cloned.1.call-start
  6.5 3.1 slice_select_fusion
  9.7 0.0 all-reduce.2.cloned.1.call-update
  9.7 0.0 all-gather.3.cloned.1.call-start
  9.7 65.3 %all-reduce.2.cloned.1.call-done = bf16[4,128,2048]{2,1,0:T(8,128)(2,1)} async-done(((bf16[4,128,2048]{2,1,0:T(8,128)(2,1)}), bf16[4,128,2048]{2,1,0:T(8,128)(2,1)}) %all-reduce.2.cloned.1.call-update) | async-done | bytes 2097168 | tf_op jit(solution)/shard_map/psum | solution.py:11
  75.1 0.0 all-gather.3.cloned.1.call-update
  75.1 0.0 all-gather.5.cloned.1.call-start
  75.2 0.0 copy-done
  75.2 1.6 copy.3
  76.7 0.0 all-gather.5.cloned.1.call-update
  76.7 0.0 reduce-scatter.2.cloned.1.call-start
  76.8 148.6 %all-gather.3.cloned.1.call-done = bf16[4,512,2048]{2,1,0:T(8,128)(2,1)} async-done(((bf16[4,128,2048]{2,1,0:T(8,128)(2,1)}), bf16[4,512,2048]{2,1,0:T(8,128)(2,1)}) %all-gather.3.cloned.1.call-update) | async-done | bytes 8388624 | tf_op jit(solution)/shard_map/all_gather | solution.py:31
  225.4 86.3 %fusion.33 = bf16[64,128,4,512]{3,0,1,2:T(8,128)(2,1)} fusion(bf16[64,128,2048,1]{2,1,0,3:T(8,128)(2,1)} %bitcast.34, bf16[4,512,2048]{2,1,0:T(8,128)(2,1)} %all-gather.3.cloned.1.call-done), kind=kOutput, calls=%fused_computation.1.clone.clone.clone.1 | convolution fusion | flops 68736253952 | bytes 75497472 | tf_op jit(solution)/shard_map/dot_general | solution.py:15
  311.7 0.0 all-gather.5.cloned.1.call-done
  311.7 24.7 %fusion.15 = f32[64,4,64]{0,2,1:T(8,128)} fusion(bf16[64,128,512]{2,0,1:T(8,128)(2,1)} %all-gather.5.cloned.1.call-done, bf16[64,128,4,512]{3,0,1,2:T(8,128)(2,1)} %fusion.33), kind=kOutput, calls=%fused_computation.8 | convolution fusion | flops 2147483648 | bytes 42008576 | tf_op jit(solution)/shard_map/dot_general | solution.py:21
  336.5 0.0 reduce-scatter.2.cloned.1.call-update
  336.5 17.8 %reduce-scatter.2.cloned.1.call-done = f32[64,4,16]{0,2,1:T(8,128)} async-done(((f32[64,4,64]{0,2,1:T(8,128)}), f32[64,4,16]{0,2,1:T(8,128)}) %reduce-scatter.2.cloned.1.call-update) | async-done | bytes 16400 | tf_op jit(solution)/shard_map/reduce_scatter | solution.py:33
Async XLA Ops:
  6.5 68.6 %copy-start = (bf16[8,128,512]{2,1,0:T(8,128)(2,1)S(1)}, bf16[8,128,512]{2,1,0:T(8,128)(2,1)}, u32[]{:S(2)}) copy-start(bf16[8,128,512]{2,1,0:T(8,128)(2,1)} %param.2) | copy-start | bytes 3145732
  6.5 68.5 %all-reduce.2.cloned.1.call-start = ((), (), s32[]{:S(2)}) async-start(), calls=%async_computation.1 | async-start | bytes 4194304 | tf_op jit(solution)/shard_map/psum | solution.py:11
  9.7 215.7 %all-gather.3.cloned.1.call-start = ((), (), s32[]{:S(2)}) async-start(), calls=%async_computation.2 | async-start | bytes 10485760 | tf_op jit(solution)/shard_map/all_gather | solution.py:31
  75.1 236.6 %all-gather.5.cloned.1.call-start = ((), (), s32[]{:S(2)}) async-start(), calls=%async_computation.3 | async-start | bytes 9437184 | tf_op jit(solution)/shard_map/all_gather | solution.py:28
  76.7 277.5 %reduce-scatter.2.cloned.1.call-start = ((), (), s32[]{:S(2)}) async-start(), calls=%async_computation.4 | async-start | bytes 163840 | tf_op jit(solution)/shard_map/reduce_scatter | solution.py:33
Sparse Core Ops, SparseCore 0:
  10.6 64.4 all-reduce.1
  76.6 148.6 all-gather.2
  227.3 54.0 all-gather.4
  336.6 17.6 reduce-scatter.1
where the time goes:
time: 361 us
  waiting for transfers between devices  232 us (64%)
  matrix products  111 us (31%)
  between operations  13.1 us (4%)
    all_gather x1, waiting for transfers between devices, per_device(): lax.all_gather(shared, 'grp', axis=1, tiled=True)  149 us
    dot_general x1, matrix products, build_tile(): lax.dot_general(chol_local, portion, (((2,), (2,)), ((), ())), preferred_...  86.3 us
    psum x1, waiting for transfers between devices, spread(): return lax.psum(kept, axis)  65.3 us
    dot_general x1, matrix products, ladder(): lax.dot_general(integrals, amp_part, (((1, 3), (1, 2)), ((), ())), prefer...  24.7 us
    reduce_scatter x1, waiting for transfers between devices, per_device(): return lax.psum_scatter(summed, 'grp', scatter_dimension=2, tiled=True)  17.8 us
  transfers between devices with their start and end apart: 4, of which 3 were waited for; matrix products, arithmetic and copies ran while one was open for 24% of the time, Pallas kernels for 0%

commit v1 on v0

--- a/solution.py
+++ b/solution.py
@@ -6,9 +6,15 @@
 A_WIN = 4
 
 
+def summed_here(value, axis):
+    pieces = lax.all_gather(value, axis, axis=0, tiled=False)
+    result = pieces.sum(axis=0)
+    return result
+
+
 def spread(value, axis, source):
     kept = jnp.where(lax.axis_index(axis) == source, value, 0).astype(value.dtype)
-    return lax.psum(kept, axis)
+    return summed_here(kept, axis)
 
 
 def build_tile(chol_local, portion):

time: 361 us -> 399 us (1.11)
  waiting for transfers between devices: 232 us -> 258 us
  other arithmetic: 3.13 us -> 14 us
    all_gather x0 -> x1, waiting for transfers between devices: none -> 92.6 us  [summed_here(): pieces = lax.all_gather(value, axis, axis=0, tiled=False)]
    psum x1 -> x0, waiting for transfers between devices: 65.3 us -> none  [spread(): return lax.psum(kept, axis)]
    reduce_sum x0 -> x1, other arithmetic: none -> 10.8 us  [summed_here(): result = pieces.sum(axis=0)]
  transfers between devices with their start and end apart: 4 -> 4, of which waited for: 3 -> 3; matrix products, arithmetic and copies ran while one was open for 24% -> 22% of each run, Pallas kernels for 0% -> 0%
where the time goes in v1:
time: 399 us; the launch traced here: 398 us
  waiting for transfers between devices  258 us (65%)
  matrix products  111 us (28%)
  other arithmetic  14 us (4%)
  between operations  13.1 us (3%)
    all_gather x1, waiting for transfers between devices, per_device(): lax.all_gather(shared, 'grp', axis=1, tiled=True)  148 us
    all_gather x1, waiting for transfers between devices, summed_here(): pieces = lax.all_gather(value, axis, axis=0, tiled=False)  92.6 us
    dot_general x1, matrix products, build_tile(): lax.dot_general(chol_local, portion, (((2,), (2,)), ((), ())), preferred_...  86.3 us
    dot_general x1, matrix products, ladder(): lax.dot_general(integrals, amp_part, (((1, 3), (1, 2)), ((), ())), prefer...  24.7 us
    reduce_scatter x1, waiting for transfers between devices, per_device(): return lax.psum_scatter(summed, 'grp', scatter_dimension=2, tiled=True)  17.8 us
    reduce_sum x1, other arithmetic, summed_here(): result = pieces.sum(axis=0)  10.8 us
  transfers between devices with their start and end apart: 4, of which 3 were waited for; matrix products, arithmetic and copies ran while one was open for 22% of the time, Pallas kernels for 0%

profile of v1, /device:TPU:0, one launch (start us, length us, event | category | flops | bytes accessed | tf_op | source)
XLA Modules:
  0.0 398.4 jit_solution(10439906688226896538)
XLA Ops:
  6.5 0.0 copy-start
  6.5 0.0 all-gather.9.cloned.1.call-start
  6.5 3.2 slice_select_fusion
  9.7 0.0 all-gather.9.cloned.1.call-update
  9.7 0.0 all-gather.5.cloned.1.call-start
  9.8 92.6 %all-gather.9.cloned.1.call-done = bf16[32,128,2048]{2,1,0:T(8,128)(2,1)} async-done(((bf16[4,128,2048]{2,1,0:T(8,128)(2,1)}), bf16[32,128,2048]{2,1,0:T(8,128)(2,1)}) %all-gather.9.cloned.1.call-update) | async-done | bytes 16777232 | tf_op jit(solution)/shard_map/all_gather | solution.py:10
  102.3 10.8 %reduce_sum.12 = bf16[4,128,2048]{2,1,0:T(8,128)(2,1)} reduce(bf16[8,4,128,2048]{3,2,1,0:T(8,128)(2,1)} %bitcast.35, bf16[]{:T(256)} %constant.9.clone.1), dimensions={0}, to_apply=%region_0.1 | reduce | flops 7340032 | bytes 18874370 | tf_op jit(solution)/shard_map/reduce_sum | solution.py:11
  113.2 0.0 all-gather.5.cloned.1.call-update
  113.2 0.0 all-gather.7.cloned.1.call-start
  113.2 0.0 copy-done
  113.2 1.6 copy.4
  114.8 0.0 all-gather.7.cloned.1.call-update
  114.8 0.0 reduce-scatter.2.cloned.1.call-start
  114.9 148.1 %all-gather.5.cloned.1.call-done = bf16[4,512,2048]{2,1,0:T(8,128)(2,1)} async-done(((bf16[4,128,2048]{2,1,0:T(8,128)(2,1)}), bf16[4,512,2048]{2,1,0:T(8,128)(2,1)}) %all-gather.5.cloned.1.call-update) | async-done | bytes 8388624 | tf_op jit(solution)/shard_map/all_gather | solution.py:37
  262.9 86.3 %fusion.33 = bf16[64,128,4,512]{3,0,1,2:T(8,128)(2,1)} fusion(bf16[64,128,2048,1]{2,1,0,3:T(8,128)(2,1)} %bitcast.36, bf16[4,512,2048]{2,1,0:T(8,128)(2,1)} %all-gather.5.cloned.1.call-done), kind=kOutput, calls=%fused_computation.1.clone.clone.clone.1 | convolution fusion | flops 68736253952 | bytes 75497472 | tf_op jit(solution)/shard_map/dot_general | solution.py:21
  349.3 0.0 all-gather.7.cloned.1.call-done
  349.3 24.7 %fusion.15 = f32[64,4,64]{0,2,1:T(8,128)} fusion(bf16[64,128,512]{2,0,1:T(8,128)(2,1)} %all-gather.7.cloned.1.call-done, bf16[64,128,4,512]{3,0,1,2:T(8,128)(2,1)} %fusion.33), kind=kOutput, calls=%fused_computation.8 | convolution fusion | flops 2147483648 | bytes 42008576 | tf_op jit(solution)/shard_map/dot_general | solution.py:27
  374.0 0.0 reduce-scatter.2.cloned.1.call-update
  374.1 17.8 %reduce-scatter.2.cloned.1.call-done = f32[64,4,16]{0,2,1:T(8,128)} async-done(((f32[64,4,64]{0,2,1:T(8,128)}), f32[64,4,16]{0,2,1:T(8,128)}) %reduce-scatter.2.cloned.1.call-update) | async-done | bytes 16400 | tf_op jit(solution)/shard_map/reduce_scatter | solution.py:39
Async XLA Ops:
  6.5 106.7 %copy-start = (bf16[8,128,512]{2,1,0:T(8,128)(2,1)S(1)}, bf16[8,128,512]{2,1,0:T(8,128)(2,1)}, u32[]{:S(2)}) copy-start(bf16[8,128,512]{2,1,0:T(8,128)(2,1)} %param.2) | copy-start | bytes 3145732
  6.5 95.8 %all-gather.9.cloned.1.call-start = ((), (), s32[]{:S(2)}) async-start(), calls=%async_computation.4 | async-start | bytes 18874368 | tf_op jit(solution)/shard_map/all_gather | solution.py:10
  9.7 253.2 %all-gather.5.cloned.1.call-start = ((), (), s32[]{:S(2)}) async-start(), calls=%async_computation.1 | async-start | bytes 10485760 | tf_op jit(solution)/shard_map/all_gather | solution.py:37
  113.2 236.1 %all-gather.7.cloned.1.call-start = ((), (), s32[]{:S(2)}) async-start(), calls=%async_computation.2 | async-start | bytes 9437184 | tf_op jit(solution)/shard_map/all_gather | solution.py:34
  114.8 277.0 %reduce-scatter.2.cloned.1.call-start = ((), (), s32[]{:S(2)}) async-start(), calls=%async_computation.3 | async-start | bytes 163840 | tf_op jit(solution)/shard_map/reduce_scatter | solution.py:39
Sparse Core Ops, SparseCore 0:
  9.8 92.4 all-gather.8
  113.3 149.5 all-gather.4
  264.8 54.0 all-gather.6
  374.2 17.6 reduce-scatter.1
